TPU v7x, 256 devices: a whole 4x4x8 slice. The times are simulated.
256 devices in a mesh: row: 8 (over z), col: 16 (over y_lo, x, core), layer: 2 (over y_hi).
Axes of the slice: x: 4, y: 4 (y_hi: 2, y_lo: 2; y = y_hi * 2 + y_lo), z: 8, core: 2. Of those that a mesh axis runs over, the one named last changes fastest.
Arguments:
- left: bfloat16 [8192, 8192], P('row', ('col', 'layer')), may hold values from -6 to 6
- middle: bfloat16 [8192, 8192], P('row', 'col'), may hold values from -0.0625 to 0.0625
- right: bfloat16 [8192, 8192], P('row', 'col'), may hold values from -0.0625 to 0.0625
Outputs:
- product: bfloat16 [8192, 8192], P('row', ('col', 'layer'))
All inputs are finite; a program needn't handle non-finite values.
Results may differ from a plain program's by a relative error of at most 0.0049.
Values may be sent and summed in bfloat16 or wider, within the bound.
A program may use at most 64 MiB of HBM per device.

v0:
```python
import jax
import jax.numpy as jnp
from jax import lax
from jax.sharding import PartitionSpec as P


def split_up(array, dim, size):
    lengths = array.shape
    blocks = array.reshape(*lengths[:dim], size, lengths[dim] // size, *lengths[dim + 1 :])
    return jnp.moveaxis(blocks, dim, 0)


def sum_at_owner(array, axis, dim):
    blocks = split_up(array, dim, lax.axis_size(axis))
    arrived = lax.all_to_all(blocks, axis, split_axis=0, concat_axis=0, tiled=True)
    return arrived.sum(axis=0)


def multiply(left, right):
    width = left.shape[1]
    layers = lax.axis_size("layer")
    layer_index = lax.axis_index("layer")
    columns = right.shape[1]
    groups = right.shape[0] // width // layers
    shaped = right.reshape(groups, layers, width, columns)
    own_rows = lax.dynamic_index_in_dim(shaped, layer_index, 1, keepdims=False).reshape(
        groups * width, columns
    )
    right_all = lax.all_gather(own_rows, "row", axis=0, tiled=True)
    return jnp.dot(
        lax.all_gather(left, "col", axis=1, tiled=True),
        right_all,
        preferred_element_type=jnp.float32,
    )


def per_device(left, middle, right):
    partial_value = multiply(left, middle)
    first = sum_at_owner(partial_value, "layer", 1)
    first = first.astype(jnp.bfloat16)
    second = multiply(first, right)
    return sum_at_owner(second, "layer", 1).astype(jnp.bfloat16)


def solution(mesh):
    return jax.shard_map(
        per_device,
        mesh=mesh,
        in_specs=(P("row", ("col", "layer")), P("row", "col"), P("row", "col")),
        out_specs=P("row", ("col", "layer")),
        check_vma=False,
    )
```

profile of v0, /device:TPU:1, one launch (start us, length us, event | category | flops | bytes accessed | tf_op | source)
XLA Modules:
  0.0 290.7 jit_solution(16866077000397679622)
XLA Ops:
  6.5 0.0 copy-start
  6.5 0.0 all-gather.5.cloned.1.call-start
  6.5 1.2 copy-done
  7.8 0.8 constant_dynamic-slice_fusion.1
  8.6 0.0 all-gather.5.cloned.1.call-update
  8.6 0.0 all-gather.7.cloned.1.call-start
  8.7 0.7 all-gather.7.cloned.1.call-update
  9.4 0.0 all-gather.11.cloned.1.call-start
  9.4 1.9 constant_dynamic-slice_fusion
  11.3 0.0 all-gather.11.cloned.1.call-update
  11.3 0.0 all-gather.9.cloned.1.call-start
  11.4 56.2 %all-gather.5.cloned.1.call-done = bf16[4096,512]{1,0:T(8,128)(2,1)} async-done(((bf16[512,512]{1,0:T(8,128)(2,1)}), bf16[4096,512]{1,0:T(8,128)(2,1)}) %all-gather.5.cloned.1.call-update) | async-done | bytes 4194320 | tf_op jit(solution)/shard_map/all_gather | solution.py:29
  67.5 64.4 %all-gather.7.cloned.1.call-done = bf16[1024,4096]{1,0:T(8,128)(2,1)} async-done(((bf16[1024,256]{1,0:T(8,128)(2,1)}), bf16[1024,4096]{1,0:T(8,128)(2,1)}) %all-gather.7.cloned.1.call-update) | async-done | bytes 8388624 | tf_op jit(solution)/shard_map/all_gather | solution.py:31
  131.9 8.2 %fusion = f32[512,1024]{1,0:T(8,128)S(1)} fusion(bf16[4096,512]{1,0:T(8,128)(2,1)} %all-gather.5.cloned.1.call-done, bf16[1024,4096]{1,0:T(8,128)(2,1)} %all-gather.7.cloned.1.call-done), kind=kOutput, calls=%fused_computation.2 | convolution fusion | flops 4294967296 | bytes 14680064 | tf_op jit(solution)/shard_map/dot_general | solution.py:30
  140.1 28.8 %all_to_all.10 = f32[2,1024,256]{1,2,0:T(8,128)S(1)} all-to-all(f32[2,1024,256]{1,2,0:T(8,128)S(1)} %bitcast.17), channel_id=1, replica_groups=mesh['row'=8,'col'=16,'layer'=2] {'layer'}, dimensions={0} | all-to-all | bytes 4194304 | tf_op jit(solution)/shard_map/all_to_all | solution.py:15
  168.9 1.1 reduce_sum.18
  170.0 0.0 all-gather.9.cloned.1.call-update
  170.0 17.7 %all-gather.11.cloned.1.call-done = bf16[4096,512]{1,0:T(8,128)(2,1)} async-done(((bf16[512,512]{1,0:T(8,128)(2,1)}), bf16[4096,512]{1,0:T(8,128)(2,1)}) %all-gather.11.cloned.1.call-update) | async-done | bytes 4194320 | tf_op jit(solution)/shard_map/all_gather | solution.py:29
  187.7 55.5 %all-gather.9.cloned.1.call-done = bf16[1024,4096]{0,1:T(8,128)(2,1)} async-done(((bf16[1024,256]{0,1:T(8,128)(2,1)}), bf16[1024,4096]{0,1:T(8,128)(2,1)}) %all-gather.9.cloned.1.call-update) | async-done | bytes 8388624 | tf_op jit(solution)/shard_map/all_gather | solution.py:31
  243.2 8.2 %fusion.1 = f32[1024,512]{0,1:T(8,128)S(1)} fusion(bf16[1024,4096]{0,1:T(8,128)(2,1)} %all-gather.9.cloned.1.call-done, bf16[4096,512]{1,0:T(8,128)(2,1)} %all-gather.11.cloned.1.call-done), kind=kOutput, calls=%fused_computation.3 | convolution fusion | flops 4294967296 | bytes 14680064 | tf_op jit(solution)/shard_map/dot_general | solution.py:30
  251.4 29.6 %all_to_all.11 = f32[2,1024,256]{1,2,0:T(8,128)S(1)} all-to-all(f32[2,1024,256]{1,2,0:T(8,128)S(1)} %bitcast.18), channel_id=1, replica_groups=mesh['row'=8,'col'=16,'layer'=2] {'layer'}, dimensions={0} | all-to-all | bytes 4194304 | tf_op jit(solution)/shard_map/all_to_all | solution.py:15
  281.0 1.1 reduce_sum.19
  282.1 2.0 copy.4
Async XLA Ops:
  6.5 1.2 copy-start
  6.5 61.0 %all-gather.5.cloned.1.call-start = ((), (), s32[]{:S(2)}) async-start(), calls=%async_computation.2 | async-start | bytes 4718592 | tf_op jit(solution)/shard_map/all_gather | solution.py:29
  8.6 123.3 %all-gather.7.cloned.1.call-start = ((), (), s32[]{:S(2)}) async-start(), calls=%async_computation.3 | async-start | bytes 8912896 | tf_op jit(solution)/shard_map/all_gather | solution.py:31
  9.4 178.3 %all-gather.11.cloned.1.call-start = ((), (), s32[]{:S(2)}) async-start(), calls=%async_computation.5 | async-start | bytes 4718592 | tf_op jit(solution)/shard_map/all_gather | solution.py:29
  11.3 231.9 %all-gather.9.cloned.1.call-start = ((), (), s32[]{:S(2)}) async-start(), calls=%async_computation.4 | async-start | bytes 8912896 | tf_op jit(solution)/shard_map/all_gather | solution.py:31
Sparse Core Ops, SparseCore 0:
  9.1 58.3 all-gather.4
  69.3 62.5 all-gather.6
  133.7 53.9 all-gather.10
  189.4 53.7 all-gather.8
where the time goes:
time: 291 us
  waiting for transfers between devices  194 us (67%)
  blocking collectives  58.3 us (20%)
  matrix products  16.5 us (6%)
  between operations  13.1 us (5%)
  local copies, waits for them, and re-layouts  5.97 us (2%)
    all_gather x2, waiting for transfers between devices, multiply(): lax.all_gather(left, 'col', axis=1, tiled=True)  120 us
    all_gather x2, waiting for transfers between devices, multiply(): right_all = lax.all_gather(own_rows, 'row', axis=0, tiled=True)  73.8 us
    all_to_all x2, blocking collectives, sum_at_owner(): lax.all_to_all(blocks, axis, split_axis=0, concat_axis=0, tiled=True)  58.3 us
    dot_general x2, matrix products, multiply(): jnp.dot(lax.all_gather(left, 'col', axis=1, tiled=True), right_all, prefe...  16.5 us
  transfers between devices with their start and end apart: 4, of which 4 were waited for; matrix products, arithmetic and copies ran while one was open for 4% of the time, Pallas kernels for 0%

commit v1 on v0

--- a/solution.py
+++ b/solution.py
@@ -2,6 +2,12 @@
 import jax.numpy as jnp
 from jax import lax
 from jax.sharding import PartitionSpec as P
+
+
+def in_order(blocks, dim):
+    blocks = jnp.moveaxis(blocks, 0, dim)
+    shape = blocks.shape
+    return blocks.reshape(*shape[:dim], shape[dim] * shape[dim + 1], *shape[dim + 2 :])
 
 
 def split_up(array, dim, size):
@@ -26,7 +32,19 @@
     own_rows = lax.dynamic_index_in_dim(shaped, layer_index, 1, keepdims=False).reshape(
         groups * width, columns
     )
-    right_all = lax.all_gather(own_rows, "row", axis=0, tiled=True)
+    count = lax.axis_size("row")
+    pairs = [(i, (i + 1) % count) for i in range(count)]
+    back = [(b, a) for a, b in pairs]
+    lower, upper = ([], [])
+    for step in range(count - 1):
+        if step % 2 == 0:
+            lower.append(lax.ppermute(lower[-1] if lower else own_rows, "row", pairs))
+        else:
+            upper.append(lax.ppermute(upper[-1] if upper else own_rows, "row", back))
+    pieces = jnp.stack([*lower[::-1], own_rows, *upper])
+    shift = lax.axis_index("row") - len(lower)
+    pieces = pieces[(jnp.arange(count) - shift) % count]
+    right_all = in_order(pieces, 0)
     return jnp.dot(
         lax.all_gather(left, "col", axis=1, tiled=True),
         right_all,

time: 291 us -> 226 us (0.78)
  the two profiles are of different devices: /device:TPU:1 before, /device:TPU:2 now
where the time goes in v1:
time: 226 us
  waiting for transfers between devices  87 us (38%)
  blocking collectives  47.7 us (21%)
  local copies, waits for them, and re-layouts  36.6 us (16%)
  starting transfers between devices  22.3 us (10%)
  matrix products  16.4 us (7%)
  between operations  13.5 us (6%)
    ppermute x8, waiting for transfers between devices, multiply(): lower.append(lax.ppermute(lower[-1] if lower else own_rows, 'row', pairs))  86.2 us
    all_to_all x2, blocking collectives, sum_at_owner(): lax.all_to_all(blocks, axis, split_axis=0, concat_axis=0, tiled=True)  47.7 us
    ppermute x6, starting transfers between devices, multiply(): upper.append(lax.ppermute(upper[-1] if upper else own_rows, 'row', back))  20.2 us
    dot_general x2, matrix products, multiply(): jnp.dot(lax.all_gather(left, 'col', axis=1, tiled=True), right_all, prefe...  16.4 us
    unnamed x16, local copies, waits for them, and re-layouts  15.4 us
    gather x2, local copies, waits for them, and re-layouts, multiply(): pieces = pieces[(jnp.arange(count) - shift) % count]  10 us
    dot_general x1, local copies, waits for them, and re-layouts, multiply(): jnp.dot(lax.all_gather(left, 'col', axis=1, tiled=True), right_all, prefe...  6.34 us
  transfers between devices with their start and end apart: 16, of which 9 were waited for; matrix products, arithmetic and copies ran while one was open for 15% of the time, Pallas kernels for 0%

profile of v1, /device:TPU:2, one launch (start us, length us, event | category | flops | bytes accessed | tf_op | source)
XLA Modules:
  0.0 225.7 jit_solution(6099649152393571983)
XLA Ops:
  7.8 2.0 collective-permute-start
  9.8 15.9 %collective-permute-done = bf16[512,512]{1,0:T(8,128)(2,1)S(1)} collective-permute-done((bf16[512,512]{1,0:T(8,128)(2,1)S(1)}, bf16[512,512]{1,0:T(8,128)(2,1)S(1)}, u32[]{:S(2)}, u32[]{:S(2)}) %collective-permute-start) | collective-permute-done | bytes 524320 | tf_op jit(solution)/shard_map/ppermute | solution.py:41
  25.7 3.2 %collective-permute-start.4 = (bf16[512,512]{1,0:T(8,128)(2,1)S(1)}, bf16[512,512]{1,0:T(8,128)(2,1)S(1)}, u32[]{:S(2)}, u32[]{:S(2)}) collective-permute-start(bf16[512,512]{1,0:T(8,128)(2,1)S(1)} %bitcast.65), channel_id=1, source_target_pairs={{32,0},{64,32},{96,64},{128,96},{160,128},{192,160},{224,192},{0,2... | collective-permute-start | bytes 1572872 | tf_op jit(solution)/shard_map/ppermute | solution.py:43
  28.9 11.1 %collective-permute-done.1 = bf16[512,512]{1,0:T(8,128)(2,1)S(1)} collective-permute-done((bf16[512,512]{1,0:T(8,128)(2,1)S(1)}, bf16[512,512]{1,0:T(8,128)(2,1)S(1)}, u32[]{:S(2)}, u32[]{:S(2)}) %collective-permute-start.1) | collective-permute-done | bytes 524320 | tf_op jit(solution)/shard_map/ppermute | solution.py:41
  40.0 3.2 %collective-permute-start.5 = (bf16[512,512]{1,0:T(8,128)(2,1)S(1)}, bf16[512,512]{1,0:T(8,128)(2,1)}, u32[]{:S(2)}, u32[]{:S(2)}) collective-permute-start(bf16[512,512]{1,0:T(8,128)(2,1)S(1)} %collective-permute-done.4), channel_id=1, source_target_pairs={{32,0},{64,32},{96,64},{128,96},{160,128},{192,160},{224,192},{0,2... | collective-permute-start | bytes 1572872 | tf_op jit(solution)/shard_map/ppermute | solution.py:43
  43.2 10.3 %collective-permute-done.2 = bf16[512,512]{1,0:T(8,128)(2,1)} collective-permute-done((bf16[512,512]{1,0:T(8,128)(2,1)S(1)}, bf16[512,512]{1,0:T(8,128)(2,1)}, u32[]{:S(2)}, u32[]{:S(2)}) %collective-permute-start.2) | collective-permute-done | bytes 524320 | tf_op jit(solution)/shard_map/ppermute | solution.py:41
  53.5 3.3 %collective-permute-start.6 = (bf16[512,512]{1,0:T(8,128)(2,1)}, bf16[512,512]{1,0:T(8,128)(2,1)S(1)}, u32[]{:S(2)}, u32[]{:S(2)}) collective-permute-start(bf16[512,512]{1,0:T(8,128)(2,1)} %collective-permute-done.5), channel_id=1, source_target_pairs={{32,0},{64,32},{96,64},{128,96},{160,128},{192,160},{224,192},{0,2... | collective-permute-start | bytes 1572872 | tf_op jit(solution)/shard_map/ppermute | solution.py:43
  56.9 9.6 %collective-permute-done.3 = bf16[512,512]{1,0:T(8,128)(2,1)} collective-permute-done((bf16[512,512]{1,0:T(8,128)(2,1)}, bf16[512,512]{1,0:T(8,128)(2,1)}, u32[]{:S(2)}, u32[]{:S(2)}) %collective-permute-start.3) | collective-permute-done | bytes 524320 | tf_op jit(solution)/shard_map/ppermute | solution.py:41
  66.4 1.9 bitcast_dynamic-update-slice_fusion.13
  76.3 4.9 %gather_fusion = bf16[8,512,512]{2,1,0:T(8,128)(2,1)} fusion(bf16[8,512,512]{2,1,0:T(8,128)(2,1)} %bitcast_dynamic-update-slice_fusion.7, s32[1024]{0:T(1024)S(1)} %pad_clamp_fusion), kind=kCustom, calls=%fused_computation | custom fusion | bytes 8388640 | tf_op jit(solution)/shard_map/gather | solution.py:46
  81.2 8.2 %fusion.7 = f32[512,1024]{1,0:T(8,128)S(1)} fusion(bf16[4096,512]{1,0:T(8,128)(2,1)} %bitcast.62, bf16[1024,4096]{1,0:T(8,128)(2,1)} %all-gather.3.cloned.1.call-done), kind=kOutput, calls=%fused_computation.30 | convolution fusion | flops 4294967296 | bytes 14680064 | tf_op jit(solution)/shard_map/dot_general | solution.py:48
  89.5 27.4 %all_to_all.10 = f32[2,1024,256]{1,2,0:T(8,128)S(1)} all-to-all(f32[2,1024,256]{1,2,0:T(8,128)S(1)} %bitcast.63), channel_id=1, replica_groups=mesh['row'=8,'col'=16,'layer'=2] {'layer'}, dimensions={0} | all-to-all | bytes 4194304 | tf_op jit(solution)/shard_map/all_to_all | solution.py:21
  118.0 2.0 copy.6
  121.2 12.1 %collective-permute-done.7 = bf16[512,512]{1,0:T(8,128)(2,1)S(1)} collective-permute-done((bf16[512,512]{1,0:T(8,128)(2,1)S(1)}, bf16[512,512]{1,0:T(8,128)(2,1)S(1)}, u32[]{:S(2)}, u32[]{:S(2)}) %collective-permute-start.7) | collective-permute-done | bytes 524320 | tf_op jit(solution)/shard_map/ppermute | solution.py:41
  133.3 3.2 %collective-permute-start.11 = (bf16[512,512]{1,0:T(8,128)(2,1)S(1)}, bf16[512,512]{1,0:T(8,128)(2,1)S(1)}, u32[]{:S(2)}, u32[]{:S(2)}) collective-permute-start(bf16[512,512]{1,0:T(8,128)(2,1)S(1)} %bitcast.68), channel_id=1, source_target_pairs={{32,0},{64,32},{96,64},{128,96},{160,128},{192,160},{224,192},{0,2... | collective-permute-start | bytes 1572872 | tf_op jit(solution)/shard_map/ppermute | solution.py:43
  136.5 9.9 %collective-permute-done.8 = bf16[512,512]{1,0:T(8,128)(2,1)S(1)} collective-permute-done((bf16[512,512]{1,0:T(8,128)(2,1)S(1)}, bf16[512,512]{1,0:T(8,128)(2,1)S(1)}, u32[]{:S(2)}, u32[]{:S(2)}) %collective-permute-start.8) | collective-permute-done | bytes 524320 | tf_op jit(solution)/shard_map/ppermute | solution.py:41
  146.4 3.5 %collective-permute-start.12 = (bf16[512,512]{1,0:T(8,128)(2,1)S(1)}, bf16[512,512]{1,0:T(8,128)(2,1)S(1)}, u32[]{:S(2)}, u32[]{:S(2)}) collective-permute-start(bf16[512,512]{1,0:T(8,128)(2,1)S(1)} %collective-permute-done.11), channel_id=1, source_target_pairs={{32,0},{64,32},{96,64},{128,96},{160,128},{192,160},{224,192},{0,2... | collective-permute-start | bytes 1572872 | tf_op jit(solution)/shard_map/ppermute | solution.py:43
  150.0 10.8 %collective-permute-done.9 = bf16[512,512]{1,0:T(8,128)(2,1)S(1)} collective-permute-done((bf16[512,512]{1,0:T(8,128)(2,1)S(1)}, bf16[512,512]{1,0:T(8,128)(2,1)S(1)}, u32[]{:S(2)}, u32[]{:S(2)}) %collective-permute-start.9) | collective-permute-done | bytes 524320 | tf_op jit(solution)/shard_map/ppermute | solution.py:41
  160.8 3.7 %collective-permute-start.13 = (bf16[512,512]{1,0:T(8,128)(2,1)S(1)}, bf16[512,512]{1,0:T(8,128)(2,1)S(1)}, u32[]{:S(2)}, u32[]{:S(2)}) collective-permute-start(bf16[512,512]{1,0:T(8,128)(2,1)S(1)} %collective-permute-done.12), channel_id=1, source_target_pairs={{32,0},{64,32},{96,64},{128,96},{160,128},{192,160},{224,192},{0,2... | collective-permute-start | bytes 1572872 | tf_op jit(solution)/shard_map/ppermute | solution.py:43
  164.5 6.6 %collective-permute-done.10 = bf16[512,512]{1,0:T(8,128)(2,1)S(1)} collective-permute-done((bf16[512,512]{1,0:T(8,128)(2,1)S(1)}, bf16[512,512]{1,0:T(8,128)(2,1)S(1)}, u32[]{:S(2)}, u32[]{:S(2)}) %collective-permute-start.10) | collective-permute-done | bytes 524320 | tf_op jit(solution)/shard_map/ppermute | solution.py:41
  177.9 5.1 %gather_fusion.1 = bf16[8,512,512]{2,1,0:T(8,128)(2,1)} fusion(bf16[8,512,512]{2,1,0:T(8,128)(2,1)} %bitcast_dynamic-update-slice_fusion, s32[1024]{0:T(1024)S(1)} %pad_clamp_fusion), kind=kCustom, calls=%fused_computation.1 | custom fusion | bytes 8388640 | tf_op jit(solution)/shard_map/gather | solution.py:46
  183.0 6.3 %copy.8 = bf16[512,4096]{1,0:T(8,128)(2,1)} copy(bf16[512,4096]{0,1:T(8,128)(2,1)} %bitcast.60) | data formatting | bytes 8388608 | tf_op jit(solution)/shard_map/dot_general | solution.py:48
  189.3 8.2 %fusion.2 = f32[2,1024,256]{2,1,0:T(8,128)S(1)} fusion(bf16[2,256,4096]{2,1,0:T(8,128)(2,1)} %bitcast.61, bf16[1024,4096]{1,0:T(8,128)(2,1)} %all-gather.5.cloned.1.call-done), kind=kOutput, calls=%fused_computation.4 | convolution fusion | flops 4294967296 | bytes 14680064 | tf_op jit(solution)/shard_map/dot_general | solution.py:48
  197.5 20.3 %all_to_all.11 = f32[2,1024,256]{2,1,0:T(8,128)S(1)} all-to-all(f32[2,1024,256]{2,1,0:T(8,128)S(1)} %fusion.2), channel_id=1, replica_groups=mesh['row'=8,'col'=16,'layer'=2] {'layer'}, dimensions={0} | all-to-all | bytes 4194304 | tf_op jit(solution)/shard_map/all_to_all | solution.py:21
  (42 shorter events, 19.4 us)
Async XLA Ops:
  6.5 1.2 copy-start
  6.5 74.7 %all-gather.3.cloned.1.call-start = ((), (), s32[]{:S(2)}) async-start(), calls=%async_computation.2 | async-start | bytes 8912896 | tf_op jit(solution)/shard_map/all_gather | solution.py:49
  7.3 182.0 %all-gather.5.cloned.1.call-start = ((), (), s32[]{:S(2)}) async-start(), calls=%async_computation.3 | async-start | bytes 8912896 | tf_op jit(solution)/shard_map/all_gather | solution.py:49
  7.8 17.9 %collective-permute-start = (bf16[512,512]{1,0:T(8,128)(2,1)S(1)}, bf16[512,512]{1,0:T(8,128)(2,1)S(1)}, u32[]{:S(2)}, u32[]{:S(2)}) collective-permute-start(bf16[512,512]{1,0:T(8,128)(2,1)S(1)} %bitcast.64), channel_id=1, source_target_pairs={{0,32},{32,64},{64,96},{96,128},{128,160},{160,192},{192,224},{224... | collective-permute-start | bytes 1572872 | tf_op jit(solution)/shard_map/ppermute | solution.py:41
  25.7 14.3 %collective-permute-start.1 = (bf16[512,512]{1,0:T(8,128)(2,1)S(1)}, bf16[512,512]{1,0:T(8,128)(2,1)S(1)}, u32[]{:S(2)}, u32[]{:S(2)}) collective-permute-start(bf16[512,512]{1,0:T(8,128)(2,1)S(1)} %collective-permute-done), channel_id=1, source_target_pairs={{0,32},{32,64},{64,96},{96,128},{128,160},{160,192},{192,224},{224... | collective-permute-start | bytes 1572872 | tf_op jit(solution)/shard_map/ppermute | solution.py:41
  25.7 14.3 %collective-permute-start.4 = (bf16[512,512]{1,0:T(8,128)(2,1)S(1)}, bf16[512,512]{1,0:T(8,128)(2,1)S(1)}, u32[]{:S(2)}, u32[]{:S(2)}) collective-permute-start(bf16[512,512]{1,0:T(8,128)(2,1)S(1)} %bitcast.65), channel_id=1, source_target_pairs={{32,0},{64,32},{96,64},{128,96},{160,128},{192,160},{224,192},{0,2... | collective-permute-start | bytes 1572872 | tf_op jit(solution)/shard_map/ppermute | solution.py:43
  40.0 13.5 %collective-permute-start.2 = (bf16[512,512]{1,0:T(8,128)(2,1)S(1)}, bf16[512,512]{1,0:T(8,128)(2,1)}, u32[]{:S(2)}, u32[]{:S(2)}) collective-permute-start(bf16[512,512]{1,0:T(8,128)(2,1)S(1)} %collective-permute-done.1), channel_id=1, source_target_pairs={{0,32},{32,64},{64,96},{96,128},{128,160},{160,192},{192,224},{224... | collective-permute-start | bytes 1572872 | tf_op jit(solution)/shard_map/ppermute | solution.py:41
  40.0 13.6 %collective-permute-start.5 = (bf16[512,512]{1,0:T(8,128)(2,1)S(1)}, bf16[512,512]{1,0:T(8,128)(2,1)}, u32[]{:S(2)}, u32[]{:S(2)}) collective-permute-start(bf16[512,512]{1,0:T(8,128)(2,1)S(1)} %collective-permute-done.4), channel_id=1, source_target_pairs={{32,0},{64,32},{96,64},{128,96},{160,128},{192,160},{224,192},{0,2... | collective-permute-start | bytes 1572872 | tf_op jit(solution)/shard_map/ppermute | solution.py:43
  53.5 12.9 %collective-permute-start.3 = (bf16[512,512]{1,0:T(8,128)(2,1)}, bf16[512,512]{1,0:T(8,128)(2,1)}, u32[]{:S(2)}, u32[]{:S(2)}) collective-permute-start(bf16[512,512]{1,0:T(8,128)(2,1)} %collective-permute-done.2), channel_id=1, source_target_pairs={{0,32},{32,64},{64,96},{96,128},{128,160},{160,192},{192,224},{224... | collective-permute-start | bytes 1572872 | tf_op jit(solution)/shard_map/ppermute | solution.py:41
  53.5 21.9 %collective-permute-start.6 = (bf16[512,512]{1,0:T(8,128)(2,1)}, bf16[512,512]{1,0:T(8,128)(2,1)S(1)}, u32[]{:S(2)}, u32[]{:S(2)}) collective-permute-start(bf16[512,512]{1,0:T(8,128)(2,1)} %collective-permute-done.5), channel_id=1, source_target_pairs={{32,0},{64,32},{96,64},{128,96},{160,128},{192,160},{224,192},{0,2... | collective-permute-start | bytes 1572872 | tf_op jit(solution)/shard_map/ppermute | solution.py:43
  121.1 12.2 %collective-permute-start.7 = (bf16[512,512]{1,0:T(8,128)(2,1)S(1)}, bf16[512,512]{1,0:T(8,128)(2,1)S(1)}, u32[]{:S(2)}, u32[]{:S(2)}) collective-permute-start(bf16[512,512]{1,0:T(8,128)(2,1)S(1)} %bitcast.67), channel_id=1, source_target_pairs={{0,32},{32,64},{64,96},{96,128},{128,160},{160,192},{192,224},{224... | collective-permute-start | bytes 1572872 | tf_op jit(solution)/shard_map/ppermute | solution.py:41
  133.3 13.1 %collective-permute-start.8 = (bf16[512,512]{1,0:T(8,128)(2,1)S(1)}, bf16[512,512]{1,0:T(8,128)(2,1)S(1)}, u32[]{:S(2)}, u32[]{:S(2)}) collective-permute-start(bf16[512,512]{1,0:T(8,128)(2,1)S(1)} %collective-permute-done.7), channel_id=1, source_target_pairs={{0,32},{32,64},{64,96},{96,128},{128,160},{160,192},{192,224},{224... | collective-permute-start | bytes 1572872 | tf_op jit(solution)/shard_map/ppermute | solution.py:41
  133.3 13.1 %collective-permute-start.11 = (bf16[512,512]{1,0:T(8,128)(2,1)S(1)}, bf16[512,512]{1,0:T(8,128)(2,1)S(1)}, u32[]{:S(2)}, u32[]{:S(2)}) collective-permute-start(bf16[512,512]{1,0:T(8,128)(2,1)S(1)} %bitcast.68), channel_id=1, source_target_pairs={{32,0},{64,32},{96,64},{128,96},{160,128},{192,160},{224,192},{0,2... | collective-permute-start | bytes 1572872 | tf_op jit(solution)/shard_map/ppermute | solution.py:43
  146.4 14.3 %collective-permute-start.9 = (bf16[512,512]{1,0:T(8,128)(2,1)S(1)}, bf16[512,512]{1,0:T(8,128)(2,1)S(1)}, u32[]{:S(2)}, u32[]{:S(2)}) collective-permute-start(bf16[512,512]{1,0:T(8,128)(2,1)S(1)} %collective-permute-done.8), channel_id=1, source_target_pairs={{0,32},{32,64},{64,96},{96,128},{128,160},{160,192},{192,224},{224... | collective-permute-start | bytes 1572872 | tf_op jit(solution)/shard_map/ppermute | solution.py:41
  146.4 14.4 %collective-permute-start.12 = (bf16[512,512]{1,0:T(8,128)(2,1)S(1)}, bf16[512,512]{1,0:T(8,128)(2,1)S(1)}, u32[]{:S(2)}, u32[]{:S(2)}) collective-permute-start(bf16[512,512]{1,0:T(8,128)(2,1)S(1)} %collective-permute-done.11), channel_id=1, source_target_pairs={{32,0},{64,32},{96,64},{128,96},{160,128},{192,160},{224,192},{0,2... | collective-permute-start | bytes 1572872 | tf_op jit(solution)/shard_map/ppermute | solution.py:43
  160.7 10.4 %collective-permute-start.10 = (bf16[512,512]{1,0:T(8,128)(2,1)S(1)}, bf16[512,512]{1,0:T(8,128)(2,1)S(1)}, u32[]{:S(2)}, u32[]{:S(2)}) collective-permute-start(bf16[512,512]{1,0:T(8,128)(2,1)S(1)} %collective-permute-done.9), channel_id=1, source_target_pairs={{0,32},{32,64},{64,96},{96,128},{128,160},{160,192},{192,224},{224... | collective-permute-start | bytes 1572872 | tf_op jit(solution)/shard_map/ppermute | solution.py:41
  160.8 16.2 %collective-permute-start.13 = (bf16[512,512]{1,0:T(8,128)(2,1)S(1)}, bf16[512,512]{1,0:T(8,128)(2,1)S(1)}, u32[]{:S(2)}, u32[]{:S(2)}) collective-permute-start(bf16[512,512]{1,0:T(8,128)(2,1)S(1)} %collective-permute-done.12), channel_id=1, source_target_pairs={{32,0},{64,32},{96,64},{128,96},{160,128},{192,160},{224,192},{0,2... | collective-permute-start | bytes 1572872 | tf_op jit(solution)/shard_map/ppermute | solution.py:43
Sparse Core Ops, SparseCore 0:
  9.1 65.8 all-gather.2
  120.2 59.6 all-gather.4
